TPU v7x, 32 devices: a whole 2x2x4 slice. The times are simulated.
32 devices in a mesh: expert: 8 (over z, core), latent: 2 (over y), row: 2 (over x).
Axes of the slice: x: 2, y: 2, z: 4, core: 2. Of those that a mesh axis runs over, the one named last changes fastest.
Arguments:
- model_acts: bfloat16 [512, 8192], P('row', 'expert'), may hold values from -6 to 6
- enc_weight: bfloat16 [8192, 12288], P('expert', ('latent', 'row')), may hold values from -0.0625 to 0.0625
- dec_weight: bfloat16 [12288, 8192], P(('latent', 'row'), 'expert'), may hold values from -0.0546875 to 0.0546875
- enc_bias: float32 [12288], P('latent'), may hold values from -3 to 3
- dec_bias: float32 [8192], P('expert'), may hold values from -3 to 3
- enc_first: bfloat16 [8192, 12288], P('expert', ('latent', 'row')), may hold values from -0.119628906 to 0.119628906
- enc_second: bfloat16 [8192, 12288], P('expert', ('latent', 'row')), may hold values from 9.9658966e-05 to 0.0099487305
- dec_first: bfloat16 [12288, 8192], P(('latent', 'row'), 'expert'), may hold values from -0.119628906 to 0.119628906
- dec_second: bfloat16 [12288, 8192], P(('latent', 'row'), 'expert'), may hold values from 9.9658966e-05 to 0.0099487305
Outputs:
- encoder_next: bfloat16 [8192, 12288], P('expert', ('latent', 'row'))
- decoder_next: bfloat16 [12288, 8192], P(('latent', 'row'), 'expert')
- enc_first_next: bfloat16 [8192, 12288], P('expert', ('latent', 'row'))
- enc_second_next: bfloat16 [8192, 12288], P('expert', ('latent', 'row'))
- dec_first_next: bfloat16 [12288, 8192], P(('latent', 'row'), 'expert')
- dec_second_next: bfloat16 [12288, 8192], P(('latent', 'row'), 'expert')
- enc_bias_grad: float32 [12288], P(('latent', 'row'))
- dec_bias_grad: float32 [8192], P('expert')
All inputs are finite; a program needn't handle non-finite values.
Results may differ from a plain program's by a relative error of at most 0.005.
Values may be sent and summed in bfloat16 or wider, within the bound.
No kernel may reach another device: no remote copies, remote signals or barrier semaphores. Data moves between devices by JAX's collectives and lax.ppermute only.
A program may use at most 128 MiB of HBM per device.

v0:
```python
import jax
import jax.numpy as jnp
from jax import lax
from jax.sharding import PartitionSpec as P

EXPERTS = 8
D = 1024
beta_one = 0.9
beta_two = 0.999
learn_rate = 0.001
adam_eps = 1e-08
bias_one = 0.9999734386011124
bias_two = 0.09520785288629115
norm_eps = 1e-06
sparsity = 1.0


def adam_step(weight, moment_one, moment_two, gradient):
    first_next = beta_one * moment_one.astype(jnp.float32) + (1.0 - beta_one) * gradient
    second_next = beta_two * moment_two.astype(jnp.float32) + (1.0 - beta_two) * gradient * gradient
    stepped = weight.astype(jnp.float32) - learn_rate * (first_next / bias_one) / (
        jnp.sqrt(second_next / bias_two) + adam_eps
    )
    return (
        stepped.astype(jnp.bfloat16),
        first_next.astype(jnp.bfloat16),
        second_next.astype(jnp.bfloat16),
    )


def contract_rows(left, right):
    return lax.dot_general(
        left, right, (((0,), (0,)), ((), ())), preferred_element_type=jnp.float32
    )


def local(
    model_acts,
    enc_weight,
    dec_weight,
    enc_bias,
    dec_bias,
    enc_first,
    enc_second,
    dec_first,
    dec_second,
):
    shard_width = model_acts.shape[1]
    local_latents = enc_weight.shape[1]
    total_rows = model_acts.shape[0] * lax.axis_size("row")
    row_index = lax.axis_index("row")
    token_rows = lax.all_gather(model_acts, "row", axis=0, tiled=True)
    bias_here = lax.dynamic_slice_in_dim(enc_bias, row_index * local_latents, local_latents)
    column_pick = (jnp.arange(EXPERTS) == lax.axis_index("expert") * shard_width // D).astype(
        jnp.float32
    )
    decoder_wide = dec_weight.astype(jnp.float32)
    partial_sq = jnp.sum(decoder_wide * decoder_wide, axis=1)
    norm_sq = lax.psum(partial_sq[:, None] * column_pick[None, :], "expert")
    decoder_norms = jnp.sqrt(norm_sq + norm_eps)
    strength = jnp.sum(decoder_norms, axis=1)
    own_norm = jnp.sum(decoder_norms * column_pick[None, :], axis=1)
    preact_part = jnp.dot(token_rows, enc_weight, preferred_element_type=jnp.float32)
    preact = lax.psum_scatter(preact_part, "expert", scatter_dimension=0, tiled=True) + bias_here
    active = preact > 0
    latent_low = lax.all_gather(
        jnp.maximum(preact, 0.0).astype(jnp.bfloat16), "expert", axis=0, tiled=True
    )
    rebuilt_part = jnp.dot(latent_low, dec_weight, preferred_element_type=jnp.float32)
    rebuilt = lax.psum(rebuilt_part, ("latent", "row"))
    grad_rows = 2.0 * (rebuilt + dec_bias - token_rows.astype(jnp.float32)) / total_rows
    grad_low = grad_rows.astype(jnp.bfloat16)
    dec_main = contract_rows(latent_low, grad_low)
    col_total = jnp.sum(latent_low.astype(jnp.float32), axis=0)
    row_bias = jnp.sum(grad_rows, axis=0)
    back_part = lax.dot_general(
        grad_low, dec_weight, (((1,), (1,)), ((), ())), preferred_element_type=jnp.float32
    )
    penalty = sparsity * strength / total_rows
    back_grad = lax.psum_scatter(back_part, "expert", scatter_dimension=0, tiled=True) + penalty
    grad_pre = lax.all_gather(
        jnp.where(active, back_grad, 0.0).astype(jnp.bfloat16), "expert", axis=0, tiled=True
    )
    enc_main = contract_rows(token_rows, grad_pre)
    bias_sum = jnp.sum(grad_pre.astype(jnp.float32), axis=0)
    dec_grad = dec_main + sparsity * (col_total / total_rows)[:, None] * (
        dec_weight.astype(jnp.float32) / own_norm[:, None]
    )
    encoder_next, enc_first_next, enc_second_next = adam_step(
        enc_weight, enc_first, enc_second, enc_main
    )
    decoder_next, dec_first_next, dec_second_next = adam_step(
        dec_weight, dec_first, dec_second, dec_grad
    )
    return (
        encoder_next,
        decoder_next,
        enc_first_next,
        enc_second_next,
        dec_first_next,
        dec_second_next,
        bias_sum,
        row_bias,
    )


def solution(mesh):
    return jax.shard_map(
        local,
        mesh=mesh,
        in_specs=(
            P("row", "expert"),
            P("expert", ("latent", "row")),
            P(("latent", "row"), "expert"),
            P("latent"),
            P("expert"),
            P("expert", ("latent", "row")),
            P("expert", ("latent", "row")),
            P(("latent", "row"), "expert"),
            P(("latent", "row"), "expert"),
        ),
        out_specs=(
            P("expert", ("latent", "row")),
            P(("latent", "row"), "expert"),
            P("expert", ("latent", "row")),
            P("expert", ("latent", "row")),
            P(("latent", "row"), "expert"),
            P(("latent", "row"), "expert"),
            P(("latent", "row")),
            P("expert"),
        ),
        check_vma=False,
    )
```

profile of v0, /device:TPU:0, one launch (start us, length us, event | category | flops | bytes accessed | tf_op | source)
XLA Modules:
  0.0 464.4 jit_solution(15385568085803733185)
XLA Ops:
  7.9 25.6 %all-gather.4.cloned.1.call-done = bf16[512,1024]{1,0:T(8,128)(2,1)} async-done(((bf16[256,1024]{1,0:T(8,128)(2,1)}), bf16[512,1024]{1,0:T(8,128)(2,1)}) %all-gather.4.cloned.1.call-update) | async-done | bytes 1048592 | tf_op jit(solution)/shard_map/all_gather | solution.py:52
  33.6 9.2 %fusion.14 = f32[512,3072]{1,0:T(8,128)} fusion(bf16[512,1024]{1,0:T(8,128)(2,1)} %all-gather.4.cloned.1.call-done, bf16[1024,3072]{1,0:T(8,128)(2,1)} %param.10), kind=kOutput, calls=%fused_computation.33 | convolution fusion | flops 3221225472 | bytes 13631488 | tf_op jit(solution)/shard_map/dot_general | solution.py:63
  43.5 69.2 %reduce-scatter.3.cloned.1.call-done = f32[64,3072]{1,0:T(8,128)} async-done(((f32[512,3072]{1,0:T(8,128)}), f32[64,3072]{1,0:T(8,128)}) %reduce-scatter.3.cloned.1.call-update) | async-done | bytes 786448 | tf_op jit(solution)/shard_map/reduce_scatter | solution.py:64
  112.7 1.9 maximum_convert_fusion
  114.7 36.9 %all-gather.6.cloned.1.call-done = bf16[512,3072]{1,0:T(8,128)(2,1)} async-done(((bf16[64,3072]{1,0:T(8,128)(2,1)}), bf16[512,3072]{1,0:T(8,128)(2,1)}) %all-gather.6.cloned.1.call-update) | async-done | bytes 3145744 | tf_op jit(solution)/shard_map/all_gather | solution.py:66
  151.7 8.5 %fusion.15 = f32[512,1024]{1,0:T(8,128)} fusion(bf16[512,3072]{1,0:T(8,128)(2,1)} %all-gather.6.cloned.1.call-done, bf16[3072,1024]{1,0:T(8,128)(2,1)} %param.11), kind=kOutput, calls=%fused_computation.34 | convolution fusion | flops 3221225472 | bytes 11534336 | tf_op jit(solution)/shard_map/dot_general | solution.py:69
  160.2 4.2 fusion
  165.2 63.5 %all-reduce.3.cloned.1.call-done = f32[512,1024]{1,0:T(8,128)} async-done(((f32[512,1024]{1,0:T(8,128)}), f32[512,1024]{1,0:T(8,128)}) %all-reduce.3.cloned.1.call-update) | async-done | bytes 2097168 | tf_op jit(solution)/shard_map/psum | solution.py:70
  228.7 2.6 fusion.11
  231.3 1.0 copy-done.4
  232.3 8.2 %fusion.16 = f32[512,3072]{1,0:T(8,128)} fusion(bf16[512,1024]{1,0:T(8,128)(2,1)S(1)} %get-tuple-element.33, bf16[3072,1024]{1,0:T(8,128)(2,1)} %param.11), kind=kOutput, calls=%fused_computation.35 | convolution fusion | flops 3221225472 | bytes 13631488 | tf_op jit(solution)/shard_map/dot_general | solution.py:76
  240.6 43.2 %all-reduce.5.cloned.1.call-done = f32[3072,8]{0,1:T(8,128)} async-done(((f32[3072,8]{0,1:T(8,128)}), f32[3072,8]{0,1:T(8,128)}) %all-reduce.5.cloned.1.call-update) | async-done | bytes 98320 | tf_op jit(solution)/shard_map/psum | solution.py:59
  283.9 1.0 multiply_reduce_fusion
  284.9 73.1 %reduce-scatter.5.cloned.1.call-done = f32[64,3072]{1,0:T(8,128)} async-done(((f32[512,3072]{1,0:T(8,128)}), f32[64,3072]{1,0:T(8,128)}) %reduce-scatter.5.cloned.1.call-update) | async-done | bytes 786448 | tf_op jit(solution)/shard_map/reduce_scatter | solution.py:80
  357.9 2.0 select_convert_fusion
  360.0 8.9 %copy.23 = bf16[1024,3072]{0,1:T(8,128)(2,1)} copy(bf16[1024,3072]{1,0:T(8,128)(2,1)} %param.10) | data formatting | bytes 12582912 | tf_op args[1]
  368.9 8.6 %copy.24 = bf16[1024,3072]{0,1:T(8,128)(2,1)} copy(bf16[1024,3072]{1,0:T(8,128)(2,1)} %param.14) | data formatting | bytes 12582912 | tf_op args[5]
  377.5 8.8 %copy.25 = bf16[1024,3072]{0,1:T(8,128)(2,1)} copy(bf16[1024,3072]{1,0:T(8,128)(2,1)} %param.15) | data formatting | bytes 12582912 | tf_op args[6]
  387.0 21.2 %fusion.9 = (bf16[3072,1024]{1,0:T(8,128)(2,1)}, bf16[3072,1024]{1,0:T(8,128)(2,1)}, bf16[3072,1024]{1,0:T(8,128)(2,1)}) fusion(bf16[3072,1024]{1,0:T(8,128)(2,1)} %param.17, bf16[3072,1024]{1,0:T(8,128)(2,1)} %param.16, bf16[3072,1024]{1,0:T(8,128)(2,1)} %param.11, f32[3072]{0:T(1024)S(1)} %get-tuple-element.24, f32[3072]{0:T(1024)S(1)} %broadcast_multiply_fusion.1, ...), kind=kOutput, calls=%fused_computation.17 | convolution fusion | flops 3287285760 | bytes 41967616 | tf_op jit(solution)/shard_map/dot_general | solution.py:32
  408.2 22.1 %fusion.10 = (bf16[1024,3072]{0,1:T(8,128)(2,1)}, bf16[1024,3072]{0,1:T(8,128)(2,1)}, bf16[1024,3072]{0,1:T(8,128)(2,1)}) fusion(bf16[1024,3072]{0,1:T(8,128)(2,1)} %copy.25, bf16[1024,3072]{0,1:T(8,128)(2,1)} %copy.24, bf16[1024,3072]{0,1:T(8,128)(2,1)} %copy.23, bf16[512,3072]{1,0:T(8,128)(2,1)} %all-gather.8.cloned.1.call-done, ...), kind=kOutput, calls=%fused_computation.18 | convolution fusion | flops 3277848576 | bytes 41943040 | tf_op jit(solution)/shard_map/dot_general | solution.py:32
  430.3 8.6 %copy.28 = bf16[1024,3072]{1,0:T(8,128)(2,1)} copy(bf16[1024,3072]{0,1:T(8,128)(2,1)} %get-tuple-element.29) | data formatting | bytes 12582912
  438.9 8.6 %copy.26 = bf16[1024,3072]{1,0:T(8,128)(2,1)} copy(bf16[1024,3072]{0,1:T(8,128)(2,1)} %get-tuple-element.30) | data formatting | bytes 12582912
  447.6 8.8 %copy.27 = bf16[1024,3072]{1,0:T(8,128)(2,1)} copy(bf16[1024,3072]{0,1:T(8,128)(2,1)} %get-tuple-element.31) | data formatting | bytes 12582912
  456.3 1.2 convert_reduce_fusion
  (34 shorter events, 3.1 us)
Async XLA Ops:
  7.2 26.4 %all-gather.4.cloned.1.call-start = ((), (), s32[]{:S(2)}) async-start(), calls=%async_computation.2 | async-start | bytes 1572864 | tf_op jit(solution)/shard_map/all_gather | solution.py:52
  7.9 104.8 %reduce-scatter.3.cloned.1.call-start = ((), (), s32[]{:S(2)}) async-start(), calls=%async_computation.3 | async-start | bytes 7077888 | tf_op jit(solution)/shard_map/reduce_scatter | solution.py:64
  42.8 0.7 copy-start.5
  42.8 108.8 %all-gather.6.cloned.1.call-start = ((), (), s32[]{:S(2)}) async-start(), calls=%async_computation.4 | async-start | bytes 3538944 | tf_op jit(solution)/shard_map/all_gather | solution.py:66
  114.7 114.0 %all-reduce.3.cloned.1.call-start = ((), (), s32[]{:S(2)}) async-start(), calls=%async_computation.5 | async-start | bytes 4194304 | tf_op jit(solution)/shard_map/psum | solution.py:70
  160.1 68.6 %copy-start.3 = (bf16[512,1024]{1,0:T(8,128)(2,1)S(1)}, bf16[512,1024]{1,0:T(8,128)(2,1)}, u32[]{:S(2)}) copy-start(bf16[512,1024]{1,0:T(8,128)(2,1)} %all-gather.4.cloned.1.call-done) | copy-start | bytes 3145732
  160.1 68.6 %copy-start.6 = (f32[1024]{0:T(1024)S(1)}, f32[1024]{0:T(1024)}, u32[]{:S(2)}) copy-start(f32[1024]{0:T(1024)} %param.13) | copy-start | bytes 12292
  160.2 123.7 %all-reduce.5.cloned.1.call-start = ((), (), s32[]{:S(2)}) async-start(), calls=%async_computation.7 | async-start | bytes 196608 | tf_op jit(solution)/shard_map/psum | solution.py:59
  165.1 192.8 %reduce-scatter.5.cloned.1.call-start = ((), (), s32[]{:S(2)}) async-start(), calls=%async_computation.6 | async-start | bytes 7077888 | tf_op jit(solution)/shard_map/reduce_scatter | solution.py:80
  231.3 1.0 copy-start.4
  240.5 117.4 %copy-start.2 = (f32[64,3072]{1,0:T(8,128)S(1)}, f32[64,3072]{1,0:T(8,128)}, u32[]{:S(2)}) copy-start(f32[64,3072]{1,0:T(8,128)} %reduce-scatter.3.cloned.1.call-done) | copy-start | bytes 2359300
  240.6 167.6 %all-gather.8.cloned.1.call-start = ((), (), s32[]{:S(2)}) async-start(), calls=%async_computation.8 | async-start | bytes 3538944 | tf_op jit(solution)/shard_map/all_gather | solution.py:81
  377.5 8.8 %copy-start = (bf16[512,3072]{1,0:T(8,128)(2,1)S(1)}, bf16[512,3072]{1,0:T(8,128)(2,1)}, u32[]{:S(2)}) copy-start(bf16[512,3072]{1,0:T(8,128)(2,1)} %all-gather.6.cloned.1.call-done) | copy-start | bytes 9437188
  447.6 8.8 %copy-start.1 = (bf16[512,3072]{1,0:T(8,128)(2,1)S(1)}, bf16[512,3072]{1,0:T(8,128)(2,1)}, u32[]{:S(2)}) copy-start(bf16[512,3072]{1,0:T(8,128)(2,1)} %all-gather.8.cloned.1.call-done) | copy-start | bytes 9437188
Sparse Core Ops, SparseCore 0:
  9.5 23.9 all-gather.3
  42.9 69.7 reduce-scatter.2
  114.9 36.6 all-gather.5
  160.3 68.3 all-reduce.2
  231.4 52.3 all-reduce.4
  286.6 71.3 reduce-scatter.4
  360.1 36.6 all-gather.7
where the time goes:
time: 466 us; the launch traced here: 464 us
  waiting for transfers between devices  312 us (67%)
  matrix products  69.3 us (15%)
  local copies, waits for them, and re-layouts  54 us (12%)
  other arithmetic  14.3 us (3%)
  between operations  14.2 us (3%)
    reduce_scatter x1, waiting for transfers between devices, local(): lax.psum_scatter(back_part, 'expert', scatter_dimension=0, tiled=True)  73.1 us
    reduce_scatter x1, waiting for transfers between devices, local(): lax.psum_scatter(preact_part, 'expert', scatter_dimension=0, tiled=True)  69.2 us
    psum x1, waiting for transfers between devices, local(): rebuilt = lax.psum(rebuilt_part, ('latent', 'row'))  63.5 us
    unnamed x20, local copies, waits for them, and re-layouts  54 us
    dot_general x2, matrix products, contract_rows(): lax.dot_general(left, right, (((0,), (0,)), ((), ())), preferred_element_...  43.4 us
    psum x1, waiting for transfers between devices, local(): norm_sq = lax.psum(partial_sq[:, None] * column_pick[None, :], 'expert')  43.2 us
    all_gather x1, waiting for transfers between devices, local(): lax.all_gather(jnp.maximum(preact, 0.0).astype(jnp.bfloat16), 'expert', a...  36.9 us
    all_gather x1, waiting for transfers between devices, local(): token_rows = lax.all_gather(model_acts, 'row', axis=0, tiled=True)  25.6 us
  transfers between devices with their start and end apart: 7, of which 6 were waited for; matrix products, arithmetic and copies ran while one was open for 14% of the time, Pallas kernels for 0%

commit v1 on v0

--- a/solution.py
+++ b/solution.py
@@ -67,7 +67,8 @@
         jnp.maximum(preact, 0.0).astype(jnp.bfloat16), "expert", axis=0, tiled=True
     )
     rebuilt_part = jnp.dot(latent_low, dec_weight, preferred_element_type=jnp.float32)
-    rebuilt = lax.psum(rebuilt_part, ("latent", "row"))
+    half = lax.psum(rebuilt_part, "row")
+    rebuilt = lax.psum(half, "latent")
     grad_rows = 2.0 * (rebuilt + dec_bias - token_rows.astype(jnp.float32)) / total_rows
     grad_low = grad_rows.astype(jnp.bfloat16)
     dec_main = contract_rows(latent_low, grad_low)

time: 466 us -> 525 us (1.13)
  waiting for transfers between devices: 312 us -> 371 us
    psum x1 -> x2, waiting for transfers between devices: 63.5 us -> 122 us  [the longest x1 62 us: local(): half = lax.psum(rebuilt_part, 'row')]
  transfers between devices with their start and end apart: 7 -> 8, of which waited for: 6 -> 7; matrix products, arithmetic and copies ran while one was open for 14% -> 12% of each run, Pallas kernels for 0% -> 0%
where the time goes in v1:
time: 525 us; the launch traced here: 523 us
  waiting for transfers between devices  371 us (71%)
  matrix products  69.3 us (13%)
  local copies, waits for them, and re-layouts  54 us (10%)
  other arithmetic  14.3 us (3%)
  between operations  14.2 us (3%)
    reduce_scatter x1, waiting for transfers between devices, local(): lax.psum_scatter(back_part, 'expert', scatter_dimension=0, tiled=True)  73.2 us
    reduce_scatter x1, waiting for transfers between devices, local(): lax.psum_scatter(preact_part, 'expert', scatter_dimension=0, tiled=True)  69.2 us
    psum x1, waiting for transfers between devices, local(): half = lax.psum(rebuilt_part, 'row')  62 us
    psum x1, waiting for transfers between devices, local(): rebuilt = lax.psum(half, 'latent')  60.2 us
    unnamed x20, local copies, waits for them, and re-layouts  54 us
    dot_general x2, matrix products, contract_rows(): lax.dot_general(left, right, (((0,), (0,)), ((), ())), preferred_element_...  43.4 us
    psum x1, waiting for transfers between devices, local(): norm_sq = lax.psum(partial_sq[:, None] * column_pick[None, :], 'expert')  43.2 us
    all_gather x1, waiting for transfers between devices, local(): lax.all_gather(jnp.maximum(preact, 0.0).astype(jnp.bfloat16), 'expert', a...  36.9 us
  transfers between devices with their start and end apart: 8, of which 7 were waited for; matrix products, arithmetic and copies ran while one was open for 12% of the time, Pallas kernels for 0%

profile of v1, /device:TPU:0, one launch (start us, length us, event | category | flops | bytes accessed | tf_op | source)
XLA Modules:
  0.0 523.2 jit_solution(6685931923984663577)
XLA Ops:
  7.9 25.6 %all-gather.4.cloned.1.call-done = bf16[512,1024]{1,0:T(8,128)(2,1)} async-done(((bf16[256,1024]{1,0:T(8,128)(2,1)}), bf16[512,1024]{1,0:T(8,128)(2,1)}) %all-gather.4.cloned.1.call-update) | async-done | bytes 1048592 | tf_op jit(solution)/shard_map/all_gather | solution.py:52
  33.6 9.2 %fusion.14 = f32[512,3072]{1,0:T(8,128)} fusion(bf16[512,1024]{1,0:T(8,128)(2,1)} %all-gather.4.cloned.1.call-done, bf16[1024,3072]{1,0:T(8,128)(2,1)} %param.10), kind=kOutput, calls=%fused_computation.33 | convolution fusion | flops 3221225472 | bytes 13631488 | tf_op jit(solution)/shard_map/dot_general | solution.py:63
  43.5 69.2 %reduce-scatter.3.cloned.1.call-done = f32[64,3072]{1,0:T(8,128)} async-done(((f32[512,3072]{1,0:T(8,128)}), f32[64,3072]{1,0:T(8,128)}) %reduce-scatter.3.cloned.1.call-update) | async-done | bytes 786448 | tf_op jit(solution)/shard_map/reduce_scatter | solution.py:64
  112.7 1.9 maximum_convert_fusion
  114.7 36.9 %all-gather.6.cloned.1.call-done = bf16[512,3072]{1,0:T(8,128)(2,1)} async-done(((bf16[64,3072]{1,0:T(8,128)(2,1)}), bf16[512,3072]{1,0:T(8,128)(2,1)}) %all-gather.6.cloned.1.call-update) | async-done | bytes 3145744 | tf_op jit(solution)/shard_map/all_gather | solution.py:66
  151.7 8.5 %fusion.15 = f32[512,1024]{1,0:T(8,128)} fusion(bf16[512,3072]{1,0:T(8,128)(2,1)} %all-gather.6.cloned.1.call-done, bf16[3072,1024]{1,0:T(8,128)(2,1)} %param.11), kind=kOutput, calls=%fused_computation.34 | convolution fusion | flops 3221225472 | bytes 11534336 | tf_op jit(solution)/shard_map/dot_general | solution.py:69
  160.2 62.0 %all-reduce.4.cloned.1.call-done = f32[512,1024]{1,0:T(8,128)} async-done(((f32[512,1024]{1,0:T(8,128)}), f32[512,1024]{1,0:T(8,128)}) %all-reduce.4.cloned.1.call-update) | async-done | bytes 2097168 | tf_op jit(solution)/shard_map/psum | solution.py:70
  222.3 4.1 fusion
  227.2 60.2 %all-reduce.6.cloned.1.call-done = f32[512,1024]{1,0:T(8,128)} async-done(((f32[512,1024]{1,0:T(8,128)}), f32[512,1024]{1,0:T(8,128)}) %all-reduce.6.cloned.1.call-update) | async-done | bytes 2097168 | tf_op jit(solution)/shard_map/psum | solution.py:71
  287.3 2.6 fusion.11
  290.9 8.2 %fusion.16 = f32[512,3072]{1,0:T(8,128)} fusion(bf16[512,1024]{1,0:T(8,128)(2,1)S(1)} %get-tuple-element.33, bf16[3072,1024]{1,0:T(8,128)(2,1)} %param.11), kind=kOutput, calls=%fused_computation.35 | convolution fusion | flops 3221225472 | bytes 13631488 | tf_op jit(solution)/shard_map/dot_general | solution.py:77
  299.2 43.2 %all-reduce.8.cloned.1.call-done = f32[3072,8]{0,1:T(8,128)} async-done(((f32[3072,8]{0,1:T(8,128)}), f32[3072,8]{0,1:T(8,128)}) %all-reduce.8.cloned.1.call-update) | async-done | bytes 98320 | tf_op jit(solution)/shard_map/psum | solution.py:59
  342.5 1.0 multiply_reduce_fusion
  343.5 73.2 %reduce-scatter.5.cloned.1.call-done = f32[64,3072]{1,0:T(8,128)} async-done(((f32[512,3072]{1,0:T(8,128)}), f32[64,3072]{1,0:T(8,128)}) %reduce-scatter.5.cloned.1.call-update) | async-done | bytes 786448 | tf_op jit(solution)/shard_map/reduce_scatter | solution.py:81
  416.7 2.0 select_convert_fusion
  418.7 8.9 %copy.23 = bf16[1024,3072]{0,1:T(8,128)(2,1)} copy(bf16[1024,3072]{1,0:T(8,128)(2,1)} %param.10) | data formatting | bytes 12582912 | tf_op args[1]
  427.6 8.6 %copy.24 = bf16[1024,3072]{0,1:T(8,128)(2,1)} copy(bf16[1024,3072]{1,0:T(8,128)(2,1)} %param.14) | data formatting | bytes 12582912 | tf_op args[5]
  436.3 8.8 %copy.25 = bf16[1024,3072]{0,1:T(8,128)(2,1)} copy(bf16[1024,3072]{1,0:T(8,128)(2,1)} %param.15) | data formatting | bytes 12582912 | tf_op args[6]
  445.7 21.2 %fusion.9 = (bf16[3072,1024]{1,0:T(8,128)(2,1)}, bf16[3072,1024]{1,0:T(8,128)(2,1)}, bf16[3072,1024]{1,0:T(8,128)(2,1)}) fusion(bf16[3072,1024]{1,0:T(8,128)(2,1)} %param.17, bf16[3072,1024]{1,0:T(8,128)(2,1)} %param.16, bf16[3072,1024]{1,0:T(8,128)(2,1)} %param.11, f32[3072]{0:T(1024)S(1)} %get-tuple-element.24, f32[3072]{0:T(1024)S(1)} %broadcast_multiply_fusion.1, ...), kind=kOutput, calls=%fused_computation.17 | convolution fusion | flops 3287285760 | bytes 41967616 | tf_op jit(solution)/shard_map/dot_general | solution.py:32
  467.0 22.1 %fusion.10 = (bf16[1024,3072]{0,1:T(8,128)(2,1)}, bf16[1024,3072]{0,1:T(8,128)(2,1)}, bf16[1024,3072]{0,1:T(8,128)(2,1)}) fusion(bf16[1024,3072]{0,1:T(8,128)(2,1)} %copy.25, bf16[1024,3072]{0,1:T(8,128)(2,1)} %copy.24, bf16[1024,3072]{0,1:T(8,128)(2,1)} %copy.23, bf16[512,3072]{1,0:T(8,128)(2,1)} %all-gather.8.cloned.1.call-done, ...), kind=kOutput, calls=%fused_computation.18 | convolution fusion | flops 3277848576 | bytes 41943040 | tf_op jit(solution)/shard_map/dot_general | solution.py:32
  489.1 8.6 %copy.28 = bf16[1024,3072]{1,0:T(8,128)(2,1)} copy(bf16[1024,3072]{0,1:T(8,128)(2,1)} %get-tuple-element.29) | data formatting | bytes 12582912
  497.7 8.6 %copy.26 = bf16[1024,3072]{1,0:T(8,128)(2,1)} copy(bf16[1024,3072]{0,1:T(8,128)(2,1)} %get-tuple-element.30) | data formatting | bytes 12582912
  506.3 8.8 %copy.27 = bf16[1024,3072]{1,0:T(8,128)(2,1)} copy(bf16[1024,3072]{0,1:T(8,128)(2,1)} %get-tuple-element.31) | data formatting | bytes 12582912
  515.1 1.2 convert_reduce_fusion
  (37 shorter events, 4.1 us)
Async XLA Ops:
  7.2 26.4 %all-gather.4.cloned.1.call-start = ((), (), s32[]{:S(2)}) async-start(), calls=%async_computation.2 | async-start | bytes 1572864 | tf_op jit(solution)/shard_map/all_gather | solution.py:52
  7.9 104.8 %reduce-scatter.3.cloned.1.call-start = ((), (), s32[]{:S(2)}) async-start(), calls=%async_computation.3 | async-start | bytes 7077888 | tf_op jit(solution)/shard_map/reduce_scatter | solution.py:64
  42.8 0.7 copy-start.5
  42.8 108.8 %all-gather.6.cloned.1.call-start = ((), (), s32[]{:S(2)}) async-start(), calls=%async_computation.4 | async-start | bytes 3538944 | tf_op jit(solution)/shard_map/all_gather | solution.py:66
  114.7 107.5 %all-reduce.4.cloned.1.call-start = ((), (), s32[]{:S(2)}) async-start(), calls=%async_computation.5 | async-start | bytes 4194304 | tf_op jit(solution)/shard_map/psum | solution.py:70
  160.1 127.2 %copy-start.3 = (bf16[512,1024]{1,0:T(8,128)(2,1)S(1)}, bf16[512,1024]{1,0:T(8,128)(2,1)}, u32[]{:S(2)}) copy-start(bf16[512,1024]{1,0:T(8,128)(2,1)} %all-gather.4.cloned.1.call-done) | copy-start | bytes 3145732
  160.1 127.2 %copy-start.6 = (f32[1024]{0:T(1024)S(1)}, f32[1024]{0:T(1024)}, u32[]{:S(2)}) copy-start(f32[1024]{0:T(1024)} %param.13) | copy-start | bytes 12292
  160.2 127.2 %all-reduce.6.cloned.1.call-start = ((), (), s32[]{:S(2)}) async-start(), calls=%async_computation.6 | async-start | bytes 4194304 | tf_op jit(solution)/shard_map/psum | solution.py:71
  222.2 120.3 %all-reduce.8.cloned.1.call-start = ((), (), s32[]{:S(2)}) async-start(), calls=%async_computation.8 | async-start | bytes 196608 | tf_op jit(solution)/shard_map/psum | solution.py:59
  227.1 189.6 %reduce-scatter.5.cloned.1.call-start = ((), (), s32[]{:S(2)}) async-start(), calls=%async_computation.7 | async-start | bytes 7077888 | tf_op jit(solution)/shard_map/reduce_scatter | solution.py:81
  290.0 1.0 copy-start.4
  299.2 117.5 %copy-start.2 = (f32[64,3072]{1,0:T(8,128)S(1)}, f32[64,3072]{1,0:T(8,128)}, u32[]{:S(2)}) copy-start(f32[64,3072]{1,0:T(8,128)} %reduce-scatter.3.cloned.1.call-done) | copy-start | bytes 2359300
  299.2 167.8 %all-gather.8.cloned.1.call-start = ((), (), s32[]{:S(2)}) async-start(), calls=%async_computation.9 | async-start | bytes 3538944 | tf_op jit(solution)/shard_map/all_gather | solution.py:82
  436.3 8.8 %copy-start = (bf16[512,3072]{1,0:T(8,128)(2,1)S(1)}, bf16[512,3072]{1,0:T(8,128)(2,1)}, u32[]{:S(2)}) copy-start(bf16[512,3072]{1,0:T(8,128)(2,1)} %all-gather.6.cloned.1.call-done) | copy-start | bytes 9437188
  506.3 8.8 %copy-start.1 = (bf16[512,3072]{1,0:T(8,128)(2,1)S(1)}, bf16[512,3072]{1,0:T(8,128)(2,1)}, u32[]{:S(2)}) copy-start(bf16[512,3072]{1,0:T(8,128)(2,1)} %all-gather.8.cloned.1.call-done) | copy-start | bytes 9437188
Sparse Core Ops, SparseCore 0:
  9.5 23.9 all-gather.3
  42.9 69.7 reduce-scatter.2
  114.9 36.6 all-gather.5
  160.3 61.8 all-reduce.3
  224.3 62.9 all-reduce.5
  290.1 52.3 all-reduce.7
  345.3 71.3 reduce-scatter.4
  418.8 36.6 all-gather.7
